TPU v7x, 32 devices: a whole 2x2x4 slice. The times are simulated.
32 devices in a mesh: patch: 16 (over z, y, x), sub: 2 (over core).
Axes of the slice: x: 2, y: 2, z: 4, core: 2. Of those that a mesh axis runs over, the one named last changes fastest.
Arguments:
- fields: float32 [5, 64, 128, 128], P(None, ('patch', 'sub')), may hold values from -6 to 6
- density: float32 [64, 128, 128], P(('patch', 'sub')), may hold values from 1 to 3
- moduli: float32 [2, 64, 128, 128], P(None, ('patch', 'sub')), may hold values from 0.5 to 128
- metric_diag: float32 [2, 64, 128, 128], P(None, ('patch', 'sub')), may hold values from 0.7 to 1.3
- metric_cross: float32 [2, 64, 128, 128], P(None, ('patch', 'sub')), may hold values from -0.3 to 0.3
- fc_extension: float32 [25, 10], replicated, may hold values from -2 to 2
- patch_count: int32 [32], P(('patch', 'sub')), may hold values from 1 to 2, as said below
- connectivity: int32 [256, 3], P(('patch', 'sub')), may hold values from -1 to 31, as said below
Outputs:
- advanced: float32 [5, 64, 128, 128], P(None, ('patch', 'sub'))
Inputs may be any that keep to these rules, and one draw needn't show every extreme that they name: `patch_count`: every device holds at most 2 live patches; the largest count is 2 in every draw. `connectivity`: links join only live slots and are symmetric with equal orientation flags on both ends; a neighbour is held by the same device or by the device whose flat index differs by 1 or 17 modulo 32; from one device to another device go at most 2 linked sides, and this number is reached in every draw.
All inputs are finite; a program needn't handle non-finite values.
Results may differ from a plain program's by a relative error of at most 0.00005.
Values sent between devices are 32-bit elements; how exact they have to be, the bound alone decides.
A program may use at most 64 MiB of HBM per device.

v0:
```python
import jax
import jax.numpy as jnp
from jax import lax
from jax.sharding import PartitionSpec as P

cfl_number = 0.5
penalty_weight = 0.5


def shifted(block, axis, distance):
    devices = range(lax.axis_size(axis))
    route = [((i - distance) % len(devices), i) for i in devices]
    return lax.ppermute(block, axis, route)


def wave_speed(density, moduli, metric_diag, metric_cross):
    stiff = moduli[0] + 2.0 * moduli[1]
    xi_norm = jnp.sqrt(metric_diag[0] * metric_diag[0] + metric_cross[0] * metric_cross[0])
    eta_norm = jnp.sqrt(metric_cross[1] * metric_cross[1] + metric_diag[1] * metric_diag[1])
    return jnp.sqrt(stiff / density) * (xi_norm + eta_norm)


def boundary_lines(state):
    stacked = jnp.stack(
        [state[:, :, 0, :], state[:, :, -1, :], state[:, :, :, 0], state[:, :, :, -1]], axis=0
    )
    return jnp.transpose(stacked, (2, 0, 1, 3))


def assemble(
    state, along_xi, along_eta, partner_lines, side_mask, density, moduli, metric_diag, metric_cross
):
    grad_x = metric_diag[0] * along_xi + metric_cross[1] * along_eta
    grad_y = metric_cross[0] * along_xi + metric_diag[1] * along_eta
    lame_first = moduli[0]
    shear = moduli[1]
    stiff = lame_first + 2.0 * shear
    rate_one = (grad_x[2] + grad_y[4]) / density
    rate_two = (grad_x[4] + grad_y[3]) / density
    rate_xx = stiff * grad_x[0] + lame_first * grad_y[1]
    rate_yy = lame_first * grad_x[0] + stiff * grad_y[1]
    rate_xy = shear * (grad_y[0] + grad_x[1])
    rate = jnp.stack([rate_one, rate_two, rate_xx, rate_yy, rate_xy], axis=0)
    points = state.shape[-1]
    jump = (
        penalty_weight
        * (points - 1)
        * (partner_lines - boundary_lines(state))
        * side_mask[:, :, None, None]
    )
    jump = jnp.transpose(jump, (1, 2, 0, 3))
    rate = rate.at[:, :, 0, :].add(jump[0])
    rate = rate.at[:, :, points - 1, :].add(jump[1])
    rate = rate.at[:, :, :, 0].add(jump[2])
    rate = rate.at[:, :, :, points - 1].add(jump[3])
    return rate


def derivative_matrix(extension, points):
    extra_cols = extension.shape[0]
    match_pts = extension.shape[1] // 2
    length = points + extra_cols
    half_len = (length - 1) // 2
    row_ids = jnp.arange(length, dtype=jnp.int32)[:, None]
    col_ids = jnp.arange(length, dtype=jnp.int32)[None, :]
    wave_ids = jnp.arange(1, half_len + 1, dtype=jnp.int32)
    phase_int = wave_ids[:, None, None] * (row_ids - col_ids)[None] % length
    angles = 2.0 * jnp.pi / length * phase_int.astype(jnp.float32)
    weights = wave_ids.astype(jnp.float32) * (2.0 * jnp.pi * (points - 1) / length)
    kernel = -(2.0 / length) * jnp.sum(weights[:, None, None] * jnp.sin(angles), axis=0)
    inner_part = kernel[:points, :points]
    outer_part = kernel[:points, points:]
    folded = jnp.dot(
        outer_part, extension, precision=lax.Precision.HIGHEST, preferred_element_type=jnp.float32
    )
    inner_part = inner_part.at[:, points - match_pts :].add(folded[:, :match_pts])
    inner_part = inner_part.at[:, :match_pts].add(folded[:, match_pts:])
    return inner_part


def shards(
    fields, density, moduli, metric_diag, metric_cross, fc_extension, patch_count, connectivity
):
    points = fields.shape[-1]
    components = fields.shape[0]
    slot_count = fields.shape[1]
    operator = derivative_matrix(fc_extension, points)
    live = jnp.arange(slot_count, dtype=jnp.int32) < patch_count[0]
    speeds = wave_speed(density, moduli, metric_diag, metric_cross)
    local_bound = jnp.max(jnp.where(live[:, None, None], speeds, jnp.float32(0.0)))
    bound = lax.pmax(local_bound, ("patch", "sub"))
    time_step = cfl_number / (bound * (points - 1))
    owner = connectivity[:, 0]
    strip_index = connectivity[:, 1]
    flipped = connectivity[:, 2] == 1
    side_mask = (owner >= 0).astype(jnp.float32).reshape(slot_count, 4)
    myself = lax.axis_index(("patch", "sub"))
    patch_total = lax.axis_size("patch")
    sub_total = lax.axis_size("sub")
    device_total = patch_total * sub_total
    far_step = device_total // 2 + 1
    positions = jnp.arange(owner.shape[0], dtype=jnp.int32)
    same_owner = owner[:, None] == owner[None, :]
    send_rank = jnp.sum(same_owner & (positions[None, :] < positions[:, None]), axis=1)
    recv_pos = jnp.sum(same_owner & (strip_index[None, :] < strip_index[:, None]), axis=1)
    line_shape = (components, points)

    def partner_lines(state):
        own_lines = boundary_lines(state).reshape((slot_count * 4,) + line_shape)
        result = own_lines[strip_index]
        for offset in (1, -1, far_step, -far_step):
            chosen = owner == (myself + offset) % device_total
            target = jnp.where(chosen, send_rank, slot_count)
            outbox = (
                jnp.zeros((slot_count,) + line_shape, jnp.float32)
                .at[target]
                .set(own_lines, mode="drop")
            )
            arrived = shifted(outbox, ("patch", "sub"), offset)
            source = owner == (myself - offset) % device_total
            result = jnp.where(
                source[:, None, None], arrived[jnp.minimum(recv_pos, slot_count - 1)], result
            )
        result = jnp.where(flipped[:, None, None], result[..., ::-1], result)
        return result.reshape((slot_count, 4) + line_shape)

    def rates(state):
        neighbours = partner_lines(state)
        along_xi = jnp.einsum("ij,cpjk->cpik", operator, state, precision=lax.Precision.HIGHEST)
        along_eta = jnp.einsum("kl,cpjl->cpjk", operator, state, precision=lax.Precision.HIGHEST)
        return assemble(
            state,
            along_xi,
            along_eta,
            neighbours,
            side_mask,
            density,
            moduli,
            metric_diag,
            metric_cross,
        )

    middle = fields + time_step * rates(fields)
    final = middle + time_step * rates(middle)
    return jnp.where(live[None, :, None, None], 0.5 * (fields + final), jnp.float32(0.0))


def solution(mesh):
    placed = (
        P(None, ("patch", "sub"), None, None),
        P(("patch", "sub"), None, None),
        P(None, ("patch", "sub"), None, None),
        P(None, ("patch", "sub"), None, None),
        P(None, ("patch", "sub"), None, None),
        P(),
        P(("patch", "sub")),
        P(("patch", "sub"), None),
    )
    return jax.shard_map(
        shards,
        mesh=mesh,
        in_specs=placed,
        out_specs=P(None, ("patch", "sub"), None, None),
        check_vma=False,
    )
```

profile of v0, /device:TPU:0, one launch (start us, length us, event | category | flops | bytes accessed | tf_op | source)
XLA Modules:
  0.0 159.0 jit_solution(11925934339036733697)
XLA Ops:
  0.0 1.7 %fusion.56 = (f32[5,2,128,1]{3,2,1,0:T(8,128)S(1)}, f32[5,2,128,1]{3,2,1,0:T(8,128)S(1)}) fusion(f32[5,2,128,128]{3,2,1,0:T(8,128)} %param.28), kind=kLoop, calls=%fused_computation.154 | loop fusion | bytes 20480 | tf_op jit(solution)/shard_map/slice | solution.py:25
  2.6 0.7 scatter_fusion
  3.3 4.4 %collective-permute-start = (f32[2,5,128]{2,1,0:T(8,128)S(1)}, f32[2,5,128]{2,1,0:T(8,128)S(1)}, u32[]{:S(2)}, u32[]{:S(2)}) collective-permute-start(f32[2,5,128]{2,1,0:T(8,128)S(1)} %scatter_fusion), channel_id=1, source_target_pairs={{17,0},{18,1},{19,2},{20,3},{21,4},{22,5},{23,6},{24,7},{25,8},{26... | collective-permute-start | bytes 15368 | tf_op jit(solution)/shard_map/ppermute | solution.py:13
  8.6 0.7 scatter_fusion.2
  9.3 5.6 %collective-permute-start.2 = (f32[2,5,128]{2,1,0:T(8,128)S(1)}, f32[2,5,128]{2,1,0:T(8,128)S(1)}, u32[]{:S(2)}, u32[]{:S(2)}) collective-permute-start(f32[2,5,128]{2,1,0:T(8,128)S(1)} %scatter_fusion.2), channel_id=1, source_target_pairs={{1,0},{2,1},{3,2},{4,3},{5,4},{6,5},{7,6},{8,7},{9,8},{10,9},{11,1... | collective-permute-start | bytes 15368 | tf_op jit(solution)/shard_map/ppermute | solution.py:13
  14.9 0.7 scatter_fusion.3
  17.6 49.5 %fusion.4 = f32[153,153]{1,0:T(8,128)S(1)} fusion(s32[153,153]{1,0:T(8,128)S(1)} %iota_subtract_fusion, s32[76]{0:T(128)S(1)} %iota_add_fusion, f32[76]{0:T(128)S(1)} %convert_multiply_fusion), kind=kLoop, calls=%fused_computation.23 | loop fusion | flops 19546516 | bytes 187880 | tf_op jit(solution)/shard_map/reduce_sum | solution.py:70
  68.4 0.7 convolution_bitcast_fusion.2
  69.5 0.8 multiply_add_fusion.4
  71.3 0.8 fusion.31
  72.3 38.4 %pmax.7 = f32[]{:T(128)} all-reduce(f32[]{:T(128)} %get-tuple-element.129), channel_id=1, replica_groups=mesh['patch'=16,'sub'=2] {'patch','sub'}, use_global_device_ids=true, to_apply=%region_1.2 | all-reduce | flops 1 | bytes 8 | tf_op jit(solution)/shard_map/pmax | solution.py:91
  115.6 4.2 %scatter-add.40 = f32[5,2,128,128]{3,2,1,0:T(8,128)S(1)} dynamic-update-slice(f32[5,2,128,128]{3,2,1,0:T(8,128)S(1)} %scatter-add.39, f32[5,2,128,1]{3,2,1,0:T(8,128)S(1)} %copy.243, s32[]{:T(128)} %constant.333.clone.1, s32[]{:T(128)} %constant.333.clone.1, s32[]{:T(128)} %constant.333.clone.1, s32[]{:T(128)} %constant.333.clone.1) | dynamic-update-slice | bytes 10244 | tf_op jit(solution)/shard_map/scatter-add | solution.py:54
  120.5 5.1 %scatter-add.41 = f32[5,2,128,128]{3,2,1,0:T(8,128)S(1)} dynamic-update-slice(f32[5,2,128,128]{3,2,1,0:T(8,128)S(1)} %scatter-add.40, f32[5,2,128,1]{3,2,1,0:T(8,128)S(1)} %copy.245, s32[]{:T(128)} %constant.333.clone.1, s32[]{:T(128)} %constant.333.clone.1, s32[]{:T(128)} %constant.333.clone.1, s32[]{:T(128)} %constant.348.clone.1) | dynamic-update-slice | bytes 10244 | tf_op jit(solution)/shard_map/scatter-add | solution.py:55
  127.4 0.8 multiply_add_fusion.1
  129.2 0.7 scatter_fusion.4
  129.9 2.8 %collective-permute-start.4 = (f32[2,5,128]{2,1,0:T(8,128)S(1)}, f32[2,5,128]{2,1,0:T(8,128)S(1)}, u32[]{:S(2)}, u32[]{:S(2)}) collective-permute-start(f32[2,5,128]{2,1,0:T(8,128)S(1)} %scatter_fusion.4), channel_id=1, source_target_pairs={{17,0},{18,1},{19,2},{20,3},{21,4},{22,5},{23,6},{24,7},{25,8},{26... | collective-permute-start | bytes 15368 | tf_op jit(solution)/shard_map/ppermute | solution.py:13
  133.5 0.7 scatter_fusion.6
  134.3 4.9 %collective-permute-start.6 = (f32[2,5,128]{2,1,0:T(8,128)S(1)}, f32[2,5,128]{2,1,0:T(8,128)S(1)}, u32[]{:S(2)}, u32[]{:S(2)}) collective-permute-start(f32[2,5,128]{2,1,0:T(8,128)S(1)} %scatter_fusion.6), channel_id=1, source_target_pairs={{1,0},{2,1},{3,2},{4,3},{5,4},{6,5},{7,6},{8,7},{9,8},{10,9},{11,1... | collective-permute-start | bytes 15368 | tf_op jit(solution)/shard_map/ppermute | solution.py:13
  139.1 0.7 scatter_fusion.7
  140.0 0.9 fusion.9
  143.3 3.3 %collective-permute-done.7 = f32[2,5,128]{2,1,0:T(8,128)S(1)} collective-permute-done((f32[2,5,128]{2,1,0:T(8,128)S(1)}, f32[2,5,128]{2,1,0:T(8,128)S(1)}, u32[]{:S(2)}, u32[]{:S(2)}) %collective-permute-start.7) | collective-permute-done | bytes 5152 | tf_op jit(solution)/shard_map/ppermute | solution.py:13
  148.1 4.2 %scatter-add.46 = f32[5,2,128,128]{3,2,1,0:T(8,128)S(1)} dynamic-update-slice(f32[5,2,128,128]{3,2,1,0:T(8,128)S(1)} %scatter-add.45, f32[5,2,128,1]{3,2,1,0:T(8,128)S(1)} %slice_add_fusion.1, s32[]{:T(128)} %constant.333.clone.1, s32[]{:T(128)} %constant.333.clone.1, s32[]{:T(128)} %constant.333.clone.1, s32[]{:T(128)} %constant.333.clone.1) | dynamic-update-slice | bytes 10244 | tf_op jit(solution)/shard_map/scatter-add | solution.py:54
  152.8 5.1 %scatter-add.49 = f32[5,2,128,128]{3,2,1,0:T(8,128)S(1)} dynamic-update-slice(f32[5,2,128,128]{3,2,1,0:T(8,128)S(1)} %scatter-add.46, f32[5,2,128,1]{3,2,1,0:T(8,128)S(1)} %slice_add_fusion, s32[]{:T(128)} %constant.333.clone.1, s32[]{:T(128)} %constant.333.clone.1, s32[]{:T(128)} %constant.333.clone.1, s32[]{:T(128)} %constant.348.clone.1) | dynamic-update-slice | bytes 10244 | tf_op jit(solution)/shard_map/scatter-add | solution.py:55
  157.9 1.1 multiply_select_fusion
  (173 shorter events, 17.9 us)
Async XLA Ops:
  0.0 67.3 %copy-start = (f32[25,10]{0,1:T(8,128)S(1)}, f32[25,10]{0,1:T(8,128)}, u32[]{:S(2)}) copy-start(f32[25,10]{0,1:T(8,128)} %param.33) | copy-start | bytes 3004
  2.5 5.2 %copy-start.24 = (s32[8]{0:T(128)}, s32[8]{0:T(128)S(1)}, u32[]{:S(2)}) copy-start(s32[8]{0:T(128)S(1)} %get-tuple-element.150) | copy-start | bytes 100
  2.5 12.4 %copy-start.20 = (s32[8]{0:T(128)}, s32[8]{0:T(128)S(1)}, u32[]{:S(2)}) copy-start(s32[8]{0:T(128)S(1)} %get-tuple-element.149) | copy-start | bytes 100
  2.5 12.4 %copy-start.22 = (s32[8]{0:T(128)}, s32[8]{0:T(128)S(1)}, u32[]{:S(2)}) copy-start(s32[8]{0:T(128)S(1)} %get-tuple-element.151) | copy-start | bytes 100
  3.3 108.8 %collective-permute-start = (f32[2,5,128]{2,1,0:T(8,128)S(1)}, f32[2,5,128]{2,1,0:T(8,128)S(1)}, u32[]{:S(2)}, u32[]{:S(2)}) collective-permute-start(f32[2,5,128]{2,1,0:T(8,128)S(1)} %scatter_fusion), channel_id=1, source_target_pairs={{17,0},{18,1},{19,2},{20,3},{21,4},{22,5},{23,6},{24,7},{25,8},{26... | collective-permute-start | bytes 15368 | tf_op jit(solution)/shard_map/ppermute | solution.py:13
  8.5 104.2 %collective-permute-start.1 = (f32[2,5,128]{2,1,0:T(8,128)S(1)}, f32[2,5,128]{2,1,0:T(8,128)S(1)}, u32[]{:S(2)}, u32[]{:S(2)}) collective-permute-start(f32[2,5,128]{2,1,0:T(8,128)S(1)} %scatter_fusion.1), channel_id=1, source_target_pairs={{15,0},{16,1},{17,2},{18,3},{19,4},{20,5},{21,6},{22,7},{23,8},{24... | collective-permute-start | bytes 15368 | tf_op jit(solution)/shard_map/ppermute | solution.py:13
  9.3 103.9 %collective-permute-start.2 = (f32[2,5,128]{2,1,0:T(8,128)S(1)}, f32[2,5,128]{2,1,0:T(8,128)S(1)}, u32[]{:S(2)}, u32[]{:S(2)}) collective-permute-start(f32[2,5,128]{2,1,0:T(8,128)S(1)} %scatter_fusion.2), channel_id=1, source_target_pairs={{1,0},{2,1},{3,2},{4,3},{5,4},{6,5},{7,6},{8,7},{9,8},{10,9},{11,1... | collective-permute-start | bytes 15368 | tf_op jit(solution)/shard_map/ppermute | solution.py:13
  15.7 98.1 %collective-permute-start.3 = (f32[2,5,128]{2,1,0:T(8,128)S(1)}, f32[2,5,128]{2,1,0:T(8,128)S(1)}, u32[]{:S(2)}, u32[]{:S(2)}) collective-permute-start(f32[2,5,128]{2,1,0:T(8,128)S(1)} %scatter_fusion.3), channel_id=1, source_target_pairs={{31,0},{0,1},{1,2},{2,3},{3,4},{4,5},{5,6},{6,7},{7,8},{8,9},{9,10... | collective-permute-start | bytes 15368 | tf_op jit(solution)/shard_map/ppermute | solution.py:13
  72.1 42.2 %copy-start.12 = (pred[8]{0:T(512)(128)(4,1)S(1)}, pred[8]{0:T(512)(128)(4,1)}, u32[]{:S(2)}) copy-start(pred[8]{0:T(512)(128)(4,1)} %get-tuple-element.153) | copy-start | bytes 28
  72.1 42.2 %copy-start.14 = (pred[8]{0:T(512)(128)(4,1)S(1)}, pred[8]{0:T(512)(128)(4,1)}, u32[]{:S(2)}) copy-start(pred[8]{0:T(512)(128)(4,1)} %get-tuple-element.154) | copy-start | bytes 28
  72.2 42.2 %copy-start.16 = (pred[8]{0:T(512)(128)(4,1)S(1)}, pred[8]{0:T(512)(128)(4,1)}, u32[]{:S(2)}) copy-start(pred[8]{0:T(512)(128)(4,1)} %get-tuple-element.155) | copy-start | bytes 28
  72.2 42.2 %copy-start.18 = (pred[8]{0:T(512)(128)(4,1)S(1)}, pred[8]{0:T(512)(128)(4,1)}, u32[]{:S(2)}) copy-start(pred[8]{0:T(512)(128)(4,1)} %get-tuple-element.156) | copy-start | bytes 28
  72.2 42.4 %copy-start.31 = (pred[8]{0:T(512)(128)(4,1)S(1)}, pred[8]{0:T(512)(128)(4,1)}, u32[]{:S(2)}) copy-start(pred[8]{0:T(512)(128)(4,1)} %compare_bitcast_fusion) | copy-start | bytes 28
  72.3 39.0 %copy-start.11 = (s32[1024]{0:T(1024)}, s32[1024]{0:T(1024)S(1)}, u32[]{:S(2)}) copy-start(s32[1024]{0:T(1024)S(1)} %get-tuple-element.162) | copy-start | bytes 12292
  128.4 10.8 %copy-start.21 = (s32[8]{0:T(128)S(1)}, s32[8]{0:T(128)}, u32[]{:S(2)}) copy-start(s32[8]{0:T(128)} %copy-done.20) | copy-start | bytes 100
  129.1 18.1 %copy-start.13 = (pred[8]{0:T(512)(128)(4,1)S(1)}, pred[8]{0:T(512)(128)(4,1)}, u32[]{:S(2)}) copy-start(pred[8]{0:T(512)(128)(4,1)} %get-tuple-element.153) | copy-start | bytes 28
  129.1 18.1 %copy-start.15 = (pred[8]{0:T(512)(128)(4,1)S(1)}, pred[8]{0:T(512)(128)(4,1)}, u32[]{:S(2)}) copy-start(pred[8]{0:T(512)(128)(4,1)} %get-tuple-element.154) | copy-start | bytes 28
  129.1 18.1 %copy-start.17 = (pred[8]{0:T(512)(128)(4,1)S(1)}, pred[8]{0:T(512)(128)(4,1)}, u32[]{:S(2)}) copy-start(pred[8]{0:T(512)(128)(4,1)} %get-tuple-element.155) | copy-start | bytes 28
  129.1 18.1 %copy-start.19 = (pred[8]{0:T(512)(128)(4,1)S(1)}, pred[8]{0:T(512)(128)(4,1)}, u32[]{:S(2)}) copy-start(pred[8]{0:T(512)(128)(4,1)} %get-tuple-element.156) | copy-start | bytes 28
  129.9 11.7 %collective-permute-start.4 = (f32[2,5,128]{2,1,0:T(8,128)S(1)}, f32[2,5,128]{2,1,0:T(8,128)S(1)}, u32[]{:S(2)}, u32[]{:S(2)}) collective-permute-start(f32[2,5,128]{2,1,0:T(8,128)S(1)} %scatter_fusion.4), channel_id=1, source_target_pairs={{17,0},{18,1},{19,2},{20,3},{21,4},{22,5},{23,6},{24,7},{25,8},{26... | collective-permute-start | bytes 15368 | tf_op jit(solution)/shard_map/ppermute | solution.py:13
  133.4 8.7 %collective-permute-start.5 = (f32[2,5,128]{2,1,0:T(8,128)S(1)}, f32[2,5,128]{2,1,0:T(8,128)S(1)}, u32[]{:S(2)}, u32[]{:S(2)}) collective-permute-start(f32[2,5,128]{2,1,0:T(8,128)S(1)} %scatter_fusion.5), channel_id=1, source_target_pairs={{15,0},{16,1},{17,2},{18,3},{19,4},{20,5},{21,6},{22,7},{23,8},{24... | collective-permute-start | bytes 15368 | tf_op jit(solution)/shard_map/ppermute | solution.py:13
  133.5 13.9 %copy-start.32 = (pred[8]{0:T(512)(128)(4,1)S(1)}, pred[8]{0:T(512)(128)(4,1)}, u32[]{:S(2)}) copy-start(pred[8]{0:T(512)(128)(4,1)} %compare_bitcast_fusion) | copy-start | bytes 28
  134.3 8.5 %collective-permute-start.6 = (f32[2,5,128]{2,1,0:T(8,128)S(1)}, f32[2,5,128]{2,1,0:T(8,128)S(1)}, u32[]{:S(2)}, u32[]{:S(2)}) collective-permute-start(f32[2,5,128]{2,1,0:T(8,128)S(1)} %scatter_fusion.6), channel_id=1, source_target_pairs={{1,0},{2,1},{3,2},{4,3},{5,4},{6,5},{7,6},{8,7},{9,8},{10,9},{11,1... | collective-permute-start | bytes 15368 | tf_op jit(solution)/shard_map/ppermute | solution.py:13
  139.9 6.7 %collective-permute-start.7 = (f32[2,5,128]{2,1,0:T(8,128)S(1)}, f32[2,5,128]{2,1,0:T(8,128)S(1)}, u32[]{:S(2)}, u32[]{:S(2)}) collective-permute-start(f32[2,5,128]{2,1,0:T(8,128)S(1)} %scatter_fusion.7), channel_id=1, source_target_pairs={{31,0},{0,1},{1,2},{2,3},{3,4},{4,5},{5,6},{6,7},{7,8},{8,9},{9,10... | collective-permute-start | bytes 15368 | tf_op jit(solution)/shard_map/ppermute | solution.py:13
  (17 other events, 33.3 us)
where the time goes:
time: 159 us
  other arithmetic  56.4 us (35%)
  blocking collectives  38.4 us (24%)
  local copies, waits for them, and re-layouts  37.4 us (24%)
  starting transfers between devices  17.9 us (11%)
  waiting for transfers between devices  3.34 us (2%)
  matrix products  3.14 us (2%)
  between operations  2.36 us (1%)
    reduce_sum x1, other arithmetic, derivative_matrix(): jnp.sum(weights[:, None, None] * jnp.sin(angles), axis=0)  49.5 us
    pmax x1, blocking collectives, shards(): bound = lax.pmax(local_bound, ('patch', 'sub'))  38.4 us
    ppermute x8, starting transfers between devices, shifted(): return lax.ppermute(block, axis, route)  17.9 us
    scatter-add x2, local copies, waits for them, and re-layouts, assemble(): rate = rate.at[:, :, :, points - 1].add(jump[3])  10.2 us
    scatter-add x2, local copies, waits for them, and re-layouts, assemble(): rate = rate.at[:, :, :, 0].add(jump[2])  8.37 us
    scatter x8, local copies, waits for them, and re-layouts, partner_lines(): outbox = jnp.zeros((slot_count,) + line_shape, jnp.float32).at[target].se...  5.9 us
    gather x8, local copies, waits for them, and re-layouts, partner_lines(): arrived[jnp.minimum(recv_pos, slot_count - 1)]  4.44 us
    ppermute x8, waiting for transfers between devices, shifted(): return lax.ppermute(block, axis, route)  3.34 us
  transfers between devices with their start and end apart: 8, of which 1 were waited for; matrix products, arithmetic and copies ran while one was open for 41% of the time, Pallas kernels for 0%

commit v1 on v0

v1 whole, which is shorter than its diff:
```python
import functools

import jax
import jax.numpy as jnp
import numpy as np
from jax import lax
from jax.experimental import pallas as pl
from jax.experimental.pallas import tpu as pltpu
from jax.sharding import PartitionSpec as P

MESH = pl.DeviceIdType.MESH
ROWS = 8
cfl_number = 0.5
penalty_weight = 0.5


def circulant(points, extra):
    length = points + extra
    half = (length - 1) // 2
    waves = np.arange(1, half + 1, dtype=np.float64)
    weights = waves * (2.0 * np.pi * (points - 1) / length)
    shifts = np.arange(length)
    phase = 2.0 * np.pi / length * (waves[:, None] * shifts[None, :] % length)
    kernel = -(2.0 / length) * np.sum(weights[:, None] * np.sin(phase), axis=0)
    at = (np.arange(points)[:, None] - np.arange(length)[None, :]) % length
    full = kernel[at].astype(np.float32)
    padded = -(-extra // ROWS) * ROWS
    outer = np.zeros((points, points), np.float32)
    outer[:, :extra] = full[:, points:]
    return full[:, :points], outer, padded


def split(x):
    hi = x.astype(jnp.bfloat16)
    lo = (x - hi.astype(jnp.float32)).astype(jnp.bfloat16)
    return hi, lo


def kernel(
    total, subs, group,
    conn, count, fields_hbm, density_hbm, moduli_hbm, diag_hbm, cross_hbm, ext, inner, outer,
    out_hbm,
    fld, den, mod, dia, cro, rate1, rate2, dxi, deta, left, right, ext_v, cols, trans, out_v,
    lines, outbox1, outbox2, inbox1, inbox2, mine1, mine2, gather1, gather2,
    load_sem, store_sem, send1, recv1, send2, recv2, msend1, mrecv1, msend2, mrecv2,
):
    comps, slots, n, _ = fld.shape
    sides = slots * 4
    chunks = n // ROWS
    me = lax.axis_index("patch") * subs + lax.axis_index("sub")
    far = total // 2 + 1
    offsets = (1, total - 1, far, total - far)
    quotient = total // group
    rank = lax.rem(me, group)
    base = me - rank
    block = lax.div(me, group)

    def place(flat):
        return (lax.div(flat, subs), lax.rem(flat, subs))

    loads = [pltpu.make_async_copy(fields_hbm, fld, load_sem.at[0])]
    for at, (src, dst) in enumerate(
        ((density_hbm, den), (moduli_hbm, mod), (diag_hbm, dia), (cross_hbm, cro))
    ):
        loads.append(pltpu.make_async_copy(src, dst, load_sem.at[at + 1]))
    for load in loads:
        load.start()

    barrier = pltpu.get_barrier_semaphore()
    near = [lax.rem(me + off, total) for off in offsets]
    first_peers = [base + lax.rem(rank + d, group) for d in range(1, group)]
    second_peers = [lax.rem(block + d, quotient) * group + rank for d in range(1, quotient)]
    everyone = near + first_peers + second_peers
    for peer in everyone:
        pl.semaphore_signal(barrier, inc=1, device_id=place(peer), device_id_type=MESH)

    owner = [conn[s, 0] for s in range(sides)]
    strip = [conn[s, 1] for s in range(sides)]
    flip = [conn[s, 2] for s in range(sides)]
    picks = []
    for peer in near:
        seen = jnp.int32(0)
        pick = [jnp.int32(0)] * slots
        for s in range(sides):
            hit = owner[s] == peer
            for k in range(slots):
                pick[k] = jnp.where(hit & (seen == k), s, pick[k])
            seen = seen + hit.astype(jnp.int32)
        picks.append(pick)
    box, local = [], []
    for s in range(sides):
        pos = jnp.int32(0)
        for t in range(sides):
            if t != s:
                pos = pos + ((owner[t] == owner[s]) & (strip[t] < strip[s])).astype(jnp.int32)
        pos = jnp.minimum(pos, slots - 1)
        at = pos
        for o, off in enumerate(offsets):
            at = jnp.where(owner[s] == lax.rem(me + total - off, total), o * slots + pos, at)
        box.append(at)
        local.append(owner[s] == me)

    lane = lax.broadcasted_iota(jnp.int32, (ROWS, n), 1)
    low, high = lane == 0, lane == n - 1
    edge = low | high
    pairs = [(f, p, p * 8 + f) for p in range(slots) for f in range(comps)]

    def collect(state):
        def columns(c, _):
            rows = pl.ds(pl.multiple_of(c * ROWS, ROWS), ROWS)
            acc = jnp.zeros((ROWS, n), jnp.float32)
            for f, p, m in pairs:
                turned = pltpu.roll(state[f, p, rows, :], 2 * m + 1, 1)
                acc = jnp.where((lane == 2 * m) | (lane == 2 * m + 1), turned, acc)
            cols[rows, :] = acc
            return _

        lax.fori_loop(0, chunks, columns, 0, unroll=4)
        trans[...] = jnp.transpose(cols[...])
        for p in range(slots):
            lines[p * 4 + 2] = trans[pl.ds(p * 16 + 1, 8, stride=2), :]
            lines[p * 4 + 3] = trans[pl.ds(p * 16, 8, stride=2), :]
            for f in range(comps):
                lines[p * 4, pl.ds(f, 1)] = state[f, p, pl.ds(0, 1), :]
                lines[p * 4 + 1, pl.ds(f, 1)] = state[f, p, pl.ds(n - 1, 1), :]

    def post(outbox, inbox, send, recv):
        for o in range(4):
            for k in range(slots):
                outbox[o, k] = lines[picks[o][k]]
        sent = []
        for o in range(4):
            copy = pltpu.make_async_remote_copy(
                src_ref=outbox.at[o],
                dst_ref=inbox.at[pl.ds(o * slots, slots)],
                send_sem=send.at[o],
                recv_sem=recv.at[o],
                device_id=place(near[o]),
                device_id_type=MESH,
            )
            copy.start()
            sent.append(copy)
        return sent

    def jumps(inbox):
        found = []
        for s in range(sides):
            partner = jnp.where(local[s], lines[strip[s]], inbox[box[s]])
            index = jnp.where(flip[s] == 1, n - 1 - lane, lane)
            partner = jnp.take_along_axis(partner, index, axis=1)
            scale = jnp.where(owner[s] >= 0, penalty_weight * (n - 1), 0.0)
            found.append(scale * (partner - lines[s]))
        return found

    def spread(jump):
        for p in range(slots):
            trans[pl.ds(p * 16 + 1, 8, stride=2), :] = jump[p * 4 + 2]
            trans[pl.ds(p * 16, 8, stride=2), :] = jump[p * 4 + 3]
        cols[...] = jnp.transpose(trans[...])

    def derive(state):
        for f in range(comps):
            h0, l0 = split(state[f, 0])
            h1, l1 = split(state[f, 1])
            rows = jnp.concatenate(
                [jnp.concatenate([h0, l0], axis=1), jnp.concatenate([h1, l1], axis=1)], axis=0
            )
            eta = jnp.dot(rows, right[...], preferred_element_type=jnp.float32)
            both = eta[:, :n] + eta[:, n:]
            deta[f, 0] = both[:n]
            deta[f, 1] = both[n:]
            body = jnp.concatenate(
                [jnp.concatenate([h0, h1], axis=1), jnp.concatenate([l0, l1], axis=1)], axis=0
            )
            xi = jnp.dot(left[...], body, preferred_element_type=jnp.float32)
            both = xi[:n] + xi[n:]
            dxi[f, 0] = both[:, :n]
            dxi[f, 1] = both[:, n:]

    def interior(rate):
        for p in range(slots):

            def body(c, _):
                rows = pl.ds(pl.multiple_of(c * ROWS, ROWS), ROWS)
                xx, yy = dia[0, p, rows, :], dia[1, p, rows, :]
                xy, ex = cro[0, p, rows, :], cro[1, p, rows, :]
                lame, shear = mod[0, p, rows, :], mod[1, p, rows, :]
                inv = den[p, rows, :]
                stiff = lame + 2.0 * shear
                ax = [dxi[f, p, rows, :] for f in range(comps)]
                ay = [deta[f, p, rows, :] for f in range(comps)]
                gx = [xx * a + ex * b for a, b in zip(ax, ay)]
                gy = [xy * a + yy * b for a, b in zip(ax, ay)]
                rate[0, p, rows, :] = (gx[2] + gy[4]) * inv
                rate[1, p, rows, :] = (gx[4] + gy[3]) * inv
                rate[2, p, rows, :] = stiff * gx[0] + lame * gy[1]
                rate[3, p, rows, :] = lame * gx[0] + stiff * gy[1]
                rate[4, p, rows, :] = shear * (gy[0] + gx[1])
                return _

            lax.fori_loop(0, chunks, body, 0, unroll=4)

    def add_rows(rate, jump):
        for p in range(slots):
            for f in range(comps):
                for side, at in ((0, 0), (1, n - 1)):
                    spot = pl.ds(at, 1)
                    rate[f, p, spot, :] = rate[f, p, spot, :] + jump[p * 4 + side][f : f + 1]

    lines[...] = jnp.zeros_like(lines)
    trans[...] = jnp.zeros_like(trans)
    ext_v[...] = jnp.zeros_like(ext_v)
    extra, twice = ext.shape
    ext_v[pl.ds(0, extra), pl.ds(0, twice)] = ext[...]
    turned = pltpu.roll(ext_v[...], n - twice // 2, 1)
    matrix = inner[...] + jnp.dot(
        outer[...], turned, precision=lax.Precision.HIGHEST, preferred_element_type=jnp.float32
    )
    hi, lo = split(matrix)
    none = jnp.zeros_like(hi)
    left[...] = jnp.concatenate(
        [jnp.concatenate([hi, hi], axis=1), jnp.concatenate([lo, none], axis=1)], axis=0
    )
    hi, lo = split(jnp.transpose(matrix))
    right[...] = jnp.concatenate(
        [jnp.concatenate([hi, lo], axis=1), jnp.concatenate([hi, none], axis=1)], axis=0
    )

    loads[0].wait()
    collect(fld)
    pl.semaphore_wait(barrier, len(everyone))
    sent1 = post(outbox1, inbox1, send1, recv1)
    derive(fld)

    for load in loads[1:]:
        load.wait()
    top = jnp.zeros((ROWS, n), jnp.float32)
    for p in range(slots):

        def speeds(c, top):
            rows = pl.ds(pl.multiple_of(c * ROWS, ROWS), ROWS)
            xx, yy = dia[0, p, rows, :], dia[1, p, rows, :]
            xy, ex = cro[0, p, rows, :], cro[1, p, rows, :]
            stiff = mod[0, p, rows, :] + 2.0 * mod[1, p, rows, :]
            inv = 1.0 / den[p, rows, :]
            den[p, rows, :] = inv
            speed = jnp.sqrt(stiff * inv) * (
                jnp.sqrt(xx * xx + xy * xy) + jnp.sqrt(ex * ex + yy * yy)
            )
            return jnp.maximum(top, speed)

        part = lax.fori_loop(
            0, chunks, speeds, jnp.zeros((ROWS, n), jnp.float32), unroll=4
        )
        top = jnp.maximum(top, jnp.where(count[0] > p, part, 0.0))

    def share(mine, gather, peers, send, recv):
        sent = []
        for d, peer in enumerate(peers):
            copy = pltpu.make_async_remote_copy(
                src_ref=mine,
                dst_ref=gather.at[d],
                send_sem=send.at[d],
                recv_sem=recv.at[d],
                device_id=place(peer),
                device_id_type=MESH,
            )
            copy.start()
            sent.append(copy)
        return sent

    mine1[...] = jnp.max(top, axis=0, keepdims=True)
    shared1 = share(mine1, gather1, first_peers, msend1, mrecv1)
    interior(rate1)

    for copy in sent1:
        copy.wait_recv()
    jump1 = jumps(inbox1)
    collect(rate1)
    for p in range(slots):
        west, east, south, north = jump1[p * 4 : p * 4 + 4]
        lines[p * 4] += (
            west + jnp.where(low, south, 0.0) + jnp.where(high, pltpu.roll(north, n - 1, 1), 0.0)
        )
        lines[p * 4 + 1] += (
            east + jnp.where(low, pltpu.roll(south, 1, 1), 0.0) + jnp.where(high, north, 0.0)
        )
        lines[p * 4 + 2] += (
            south + jnp.where(low, west, 0.0) + jnp.where(high, pltpu.roll(east, n - 1, 1), 0.0)
        )
        lines[p * 4 + 3] += (
            north + jnp.where(low, pltpu.roll(west, 1, 1), 0.0) + jnp.where(high, east, 0.0)
        )
    sent2 = post(outbox2, inbox2, send2, recv2)

    for copy in shared1:
        copy.wait_recv()
    best = mine1[...]
    for d in range(len(first_peers)):
        best = jnp.maximum(best, gather1[d])
    mine2[...] = best
    shared2 = share(mine2, gather2, second_peers, msend2, mrecv2)

    spread(jump1)
    add_rows(rate1, jump1)

    def patch_up(c, _):
        rows = pl.ds(pl.multiple_of(c * ROWS, ROWS), ROWS)
        both = cols[rows, :]
        for f, p, m in pairs:
            side = pltpu.roll(both, n - (2 * m + 1), 1)
            rate1[f, p, rows, :] = rate1[f, p, rows, :] + jnp.where(edge, side, 0.0)
        return _

    lax.fori_loop(0, chunks, patch_up, 0, unroll=4)
    derive(rate1)
    interior(rate2)

    for copy in shared2:
        copy.wait_recv()
    for d in range(len(second_peers)):
        best = jnp.maximum(best, gather2[d])
    bound = jnp.max(best, axis=1, keepdims=True)
    step = jnp.broadcast_to(cfl_number / (bound * (n - 1)), (ROWS, n))
    half = 0.5 * step * step

    for copy in sent2:
        copy.wait_recv()
    jump2 = jumps(inbox2)
    spread(jump2)
    add_rows(rate2, jump2)
    stores = []
    for p in range(slots):
        live = count[0] > p

        def finish(c, _):
            rows = pl.ds(pl.multiple_of(c * ROWS, ROWS), ROWS)
            both = cols[rows, :]
            for f in range(comps):
                side = pltpu.roll(both, n - (2 * (p * 8 + f) + 1), 1)
                second = rate2[f, p, rows, :] + jnp.where(edge, side, 0.0)
                value = fld[f, p, rows, :] + step * rate1[f, p, rows, :] + half * second
                out_v[f, p, rows, :] = jnp.where(live, value, 0.0)
            return _

        lax.fori_loop(0, chunks, finish, 0, unroll=4)
        store = pltpu.make_async_copy(out_v.at[:, p], out_hbm.at[:, p], store_sem.at[p])
        store.start()
        stores.append(store)
    for copy in sent1 + sent2 + shared1 + shared2:
        copy.wait_send()
    for store in stores:
        store.wait()


def shards(
    total, subs, fields, density, moduli, metric_diag, metric_cross, extension, count, connectivity
):
    comps, slots, n, _ = fields.shape
    group = max(g for g in range(1, total) if total % g == 0 and g * g <= total)
    inner, outer, _ = circulant(n, extension.shape[0])
    f32 = jnp.float32
    vmem = pl.BlockSpec(memory_space=pltpu.VMEM)
    smem = pl.BlockSpec(memory_space=pltpu.SMEM)
    hbm = pl.BlockSpec(memory_space=pl.ANY)
    state = pltpu.VMEM(fields.shape, f32)
    dma = pltpu.SemaphoreType.DMA
    boxed = pltpu.VMEM((4, slots, 8, n), f32)
    arrived = pltpu.VMEM((4 * slots, 8, n), f32)
    quotient = total // group
    return pl.pallas_call(
        functools.partial(kernel, total, subs, group),
        out_shape=jax.ShapeDtypeStruct(fields.shape, f32),
        in_specs=[smem, smem] + [hbm] * 5 + [vmem] * 3,
        out_specs=hbm,
        scratch_shapes=[
            state,
            pltpu.VMEM(density.shape, f32),
            pltpu.VMEM(moduli.shape, f32),
            pltpu.VMEM(metric_diag.shape, f32),
            pltpu.VMEM(metric_cross.shape, f32),
            state, state, state, state,
            pltpu.VMEM((2 * n, 2 * n), jnp.bfloat16),
            pltpu.VMEM((2 * n, 2 * n), jnp.bfloat16),
            pltpu.VMEM((n, n), f32),
            pltpu.VMEM((n, n), f32),
            pltpu.VMEM((n, n), f32),
            state,
            pltpu.VMEM((slots * 4, 8, n), f32),
            boxed, boxed, arrived, arrived,
            pltpu.VMEM((1, n), f32),
            pltpu.VMEM((1, n), f32),
            pltpu.VMEM((group - 1, 1, n), f32),
            pltpu.VMEM((quotient - 1, 1, n), f32),
            dma((5,)), dma((slots,)),
            dma((4,)), dma((4,)), dma((4,)), dma((4,)),
            dma((group - 1,)), dma((group - 1,)), dma((quotient - 1,)), dma((quotient - 1,)),
        ],
        compiler_params=pltpu.CompilerParams(collective_id=0, has_side_effects=True),
    )(connectivity, count, fields, density, moduli, metric_diag, metric_cross, extension,
      jnp.asarray(inner), jnp.asarray(outer))


def solution(mesh):
    placed = (
        P(None, ("patch", "sub"), None, None),
        P(("patch", "sub"), None, None),
        P(None, ("patch", "sub"), None, None),
        P(None, ("patch", "sub"), None, None),
        P(None, ("patch", "sub"), None, None),
        P(),
        P(("patch", "sub")),
        P(("patch", "sub"), None),
    )
    total = mesh.shape["patch"] * mesh.shape["sub"]
    return jax.shard_map(
        functools.partial(shards, total, mesh.shape["sub"]),
        mesh=mesh,
        in_specs=placed,
        out_specs=P(None, ("patch", "sub"), None, None),
        check_vma=False,
    )
```

time: 159 us -> 23.7 us (0.15)
  other arithmetic: 56.4 us -> 0 us
  blocking collectives: 38.4 us -> 0 us
  local copies, waits for them, and re-layouts: 37.4 us -> 4.69 us
  Pallas kernels: 0 us -> 18 us
  starting transfers between devices: 17.9 us -> 0 us
  waiting for transfers between devices: 3.34 us -> 0 us
  matrix products: 3.14 us -> 0 us
  between operations: 2.36 us -> 0.66 us
    reduce_sum x2 -> x0, other arithmetic: 49.7 us -> none  [the longest x1 49.5 us: derivative_matrix(): jnp.sum(weights[:, None, None] * jnp.sin(angles), axis=0)]
    pmax x1 -> x0, blocking collectives: 38.4 us -> none  [shards(): bound = lax.pmax(local_bound, ('patch', 'sub'))]
    scatter-add x10 -> x0, local copies, waits for them, and re-layouts: 19.2 us -> none  [the longest x2 10.2 us: assemble(): rate = rate.at[:, :, :, points - 1].add(jump[3])]
    pallas_call x0 -> x1, Pallas kernels: none -> 18 us  [shards(): pl.pallas_call(functools.partial(kernel, total, subs, group), out_shape=j...]
    ppermute x8 -> x0, starting transfers between devices: 17.9 us -> none  [shifted(): return lax.ppermute(block, axis, route)]
    scatter x8 -> x0, local copies, waits for them, and re-layouts: 5.9 us -> none  [partner_lines(): outbox = jnp.zeros((slot_count,) + line_shape, jnp.float32).at[target].se...]
    gather x10 -> x0, local copies, waits for them, and re-layouts: 5.67 us -> none  [the longest x8 4.44 us: partner_lines(): arrived[jnp.minimum(recv_pos, slot_count - 1)]]
    ppermute x8 -> x0, waiting for transfers between devices: 3.34 us -> none  [shifted(): return lax.ppermute(block, axis, route)]
  transfers between devices with their start and end apart: 8 -> 0, of which waited for: 1 -> 0; matrix products, arithmetic and copies ran while one was open for 41% -> 0% of each run, Pallas kernels for 0% -> 0%
where the time goes in v1:
time: 23.7 us; the launch traced here: 23.4 us
  Pallas kernels  18 us (76%)
  local copies, waits for them, and re-layouts  4.69 us (20%)
  between operations  0.66 us (3%)
    pallas_call x1, Pallas kernels, shards(): pl.pallas_call(functools.partial(kernel, total, subs, group), out_shape=j...  18 us
    unnamed x3, local copies, waits for them, and re-layouts  4.69 us

profile of v1, /device:TPU:0, one launch (start us, length us, event | category | flops | bytes accessed | tf_op | source)
XLA Modules:
  0.0 23.4 jit_solution(16094884448137401377)
XLA Ops:
  0.7 1.3 %copy.11.conn = s32[8,3]{1,0:T(8,128)} copy(s32[8,3]{0,1:T(4,128)} %param.17) | data formatting | bytes 192 | tf_op args[7]
  2.0 1.4 %copy.12.ext = f32[25,10]{1,0:T(8,128)} copy(f32[25,10]{0,1:T(8,128)} %param.15) | data formatting | bytes 2000 | tf_op args[5]
  3.4 18.0 %shard_map.100 = f32[5,2,128,128]{3,2,1,0:T(8,128)} custom-call(s32[8,3]{1,0:T(8,128)} %copy.11.conn, s32[1]{0:T(128)S(6)} %copy.14.count, f32[5,2,128,128]{3,2,1,0:T(8,128)} %fields_hbm.1, f32[2,128,128]{2,1,0:T(8,128)} %density_hbm.1, f32[2,2,128,128]{3,2,1,0:T(8,128)} %moduli_hbm.1, f32[2,2,128,128]{3,2,1,0:T(8,128)} %diag_hbm.1, ...), custom_call_target="tpu_custom_call" | custom-call | tf_op jit(solution)/shard_map/pallas_call | solution.py:371
  21.4 2.0 %copy.15 = f32[5,2,128,128]{3,2,1,0:T(8,128)} copy(f32[5,2,128,128]{3,2,1,0:T(8,128)} %shard_map.100) | data formatting | bytes 1310720

commit v2 on v1

--- a/solution.py
+++ b/solution.py
@@ -39,10 +39,10 @@
 def kernel(
     total, subs, group,
     conn, count, fields_hbm, density_hbm, moduli_hbm, diag_hbm, cross_hbm, ext, inner, outer,
-    out_hbm,
-    fld, den, mod, dia, cro, rate1, rate2, dxi, deta, left, right, ext_v, cols, trans, out_v,
-    lines, outbox1, outbox2, inbox1, inbox2, mine1, mine2, gather1, gather2,
-    load_sem, store_sem, send1, recv1, send2, recv2, msend1, mrecv1, msend2, mrecv2,
+    out_v,
+    fld, den, mod, dia, cro, rate1, rate2, dxi, deta, left, right, ext_v, cols, trans,
+    lines, lines2, outbox1, outbox2, inbox1, inbox2, mine1, mine2, gather1, gather2,
+    load_sem, send1, recv1, send2, recv2, msend1, mrecv1, msend2, mrecv2,
 ):
     comps, slots, n, _ = fld.shape
     sides = slots * 4
@@ -74,9 +74,9 @@
     for peer in everyone:
         pl.semaphore_signal(barrier, inc=1, device_id=place(peer), device_id_type=MESH)
 
-    owner = [conn[s, 0] for s in range(sides)]
-    strip = [conn[s, 1] for s in range(sides)]
-    flip = [conn[s, 2] for s in range(sides)]
+    owner = [conn[0, s] for s in range(sides)]
+    strip = [conn[1, s] for s in range(sides)]
+    flip = [conn[2, s] for s in range(sides)]
     picks = []
     for peer in near:
         seen = jnp.int32(0)
@@ -105,7 +105,7 @@
     edge = low | high
     pairs = [(f, p, p * 8 + f) for p in range(slots) for f in range(comps)]
 
-    def collect(state):
+    def collect(state, lines):
         def columns(c, _):
             rows = pl.ds(pl.multiple_of(c * ROWS, ROWS), ROWS)
             acc = jnp.zeros((ROWS, n), jnp.float32)
@@ -124,7 +124,7 @@
                 lines[p * 4, pl.ds(f, 1)] = state[f, p, pl.ds(0, 1), :]
                 lines[p * 4 + 1, pl.ds(f, 1)] = state[f, p, pl.ds(n - 1, 1), :]
 
-    def post(outbox, inbox, send, recv):
+    def post(lines, outbox, inbox, send, recv):
         for o in range(4):
             for k in range(slots):
                 outbox[o, k] = lines[picks[o][k]]
@@ -142,7 +142,7 @@
             sent.append(copy)
         return sent
 
-    def jumps(inbox):
+    def jumps(lines, inbox):
         found = []
         for s in range(sides):
             partner = jnp.where(local[s], lines[strip[s]], inbox[box[s]])
@@ -208,13 +208,18 @@
                     rate[f, p, spot, :] = rate[f, p, spot, :] + jump[p * 4 + side][f : f + 1]
 
     lines[...] = jnp.zeros_like(lines)
+    lines2[...] = jnp.zeros_like(lines2)
     trans[...] = jnp.zeros_like(trans)
     ext_v[...] = jnp.zeros_like(ext_v)
-    extra, twice = ext.shape
-    ext_v[pl.ds(0, extra), pl.ds(0, twice)] = ext[...]
-    turned = pltpu.roll(ext_v[...], n - twice // 2, 1)
-    matrix = inner[...] + jnp.dot(
-        outer[...], turned, precision=lax.Precision.HIGHEST, preferred_element_type=jnp.float32
+    twice, extra = ext.shape
+    ext_v[pl.ds(0, twice), pl.ds(0, extra)] = ext[...]
+    turned = pltpu.roll(ext_v[...], n - twice // 2, 0)
+    matrix = inner[...] + lax.dot_general(
+        outer[...],
+        turned,
+        (((1,), (1,)), ((), ())),
+        precision=lax.Precision.HIGHEST,
+        preferred_element_type=jnp.float32,
     )
     hi, lo = split(matrix)
     none = jnp.zeros_like(hi)
@@ -227,9 +232,9 @@
     )
 
     loads[0].wait()
-    collect(fld)
+    collect(fld, lines)
     pl.semaphore_wait(barrier, len(everyone))
-    sent1 = post(outbox1, inbox1, send1, recv1)
+    sent1 = post(lines, outbox1, inbox1, send1, recv1)
     derive(fld)
 
     for load in loads[1:]:
@@ -273,25 +278,25 @@
     shared1 = share(mine1, gather1, first_peers, msend1, mrecv1)
     interior(rate1)
 
+    collect(rate1, lines2)
     for copy in sent1:
         copy.wait_recv()
-    jump1 = jumps(inbox1)
-    collect(rate1)
+    jump1 = jumps(lines, inbox1)
     for p in range(slots):
         west, east, south, north = jump1[p * 4 : p * 4 + 4]
-        lines[p * 4] += (
+        lines2[p * 4] += (
             west + jnp.where(low, south, 0.0) + jnp.where(high, pltpu.roll(north, n - 1, 1), 0.0)
         )
-        lines[p * 4 + 1] += (
+        lines2[p * 4 + 1] += (
             east + jnp.where(low, pltpu.roll(south, 1, 1), 0.0) + jnp.where(high, north, 0.0)
         )
-        lines[p * 4 + 2] += (
+        lines2[p * 4 + 2] += (
             south + jnp.where(low, west, 0.0) + jnp.where(high, pltpu.roll(east, n - 1, 1), 0.0)
         )
-        lines[p * 4 + 3] += (
+        lines2[p * 4 + 3] += (
             north + jnp.where(low, pltpu.roll(west, 1, 1), 0.0) + jnp.where(high, east, 0.0)
         )
-    sent2 = post(outbox2, inbox2, send2, recv2)
+    sent2 = post(lines2, outbox2, inbox2, send2, recv2)
 
     for copy in shared1:
         copy.wait_recv()
@@ -326,10 +331,9 @@
 
     for copy in sent2:
         copy.wait_recv()
-    jump2 = jumps(inbox2)
+    jump2 = jumps(lines2, inbox2)
     spread(jump2)
     add_rows(rate2, jump2)
-    stores = []
     for p in range(slots):
         live = count[0] > p
 
@@ -344,13 +348,8 @@
             return _
 
         lax.fori_loop(0, chunks, finish, 0, unroll=4)
-        store = pltpu.make_async_copy(out_v.at[:, p], out_hbm.at[:, p], store_sem.at[p])
-        store.start()
-        stores.append(store)
     for copy in sent1 + sent2 + shared1 + shared2:
         copy.wait_send()
-    for store in stores:
-        store.wait()
 
 
 def shards(
@@ -362,7 +361,7 @@
     f32 = jnp.float32
     vmem = pl.BlockSpec(memory_space=pltpu.VMEM)
     smem = pl.BlockSpec(memory_space=pltpu.SMEM)
-    hbm = pl.BlockSpec(memory_space=pl.ANY)
+    hbm = pl.BlockSpec(memory_space=pltpu.HBM)
     state = pltpu.VMEM(fields.shape, f32)
     dma = pltpu.SemaphoreType.DMA
     boxed = pltpu.VMEM((4, slots, 8, n), f32)
@@ -370,9 +369,9 @@
     quotient = total // group
     return pl.pallas_call(
         functools.partial(kernel, total, subs, group),
-        out_shape=jax.ShapeDtypeStruct(fields.shape, f32),
+        out_shape=pltpu.VMEM(fields.shape, f32),
         in_specs=[smem, smem] + [hbm] * 5 + [vmem] * 3,
-        out_specs=hbm,
+        out_specs=vmem,
         scratch_shapes=[
             state,
             pltpu.VMEM(density.shape, f32),
@@ -385,19 +384,19 @@
             pltpu.VMEM((n, n), f32),
             pltpu.VMEM((n, n), f32),
             pltpu.VMEM((n, n), f32),
-            state,
+            pltpu.VMEM((slots * 4, 8, n), f32),
             pltpu.VMEM((slots * 4, 8, n), f32),
             boxed, boxed, arrived, arrived,
             pltpu.VMEM((1, n), f32),
             pltpu.VMEM((1, n), f32),
             pltpu.VMEM((group - 1, 1, n), f32),
             pltpu.VMEM((quotient - 1, 1, n), f32),
-            dma((5,)), dma((slots,)),
+            dma((5,)),
             dma((4,)), dma((4,)), dma((4,)), dma((4,)),
             dma((group - 1,)), dma((group - 1,)), dma((quotient - 1,)), dma((quotient - 1,)),
         ],
         compiler_params=pltpu.CompilerParams(collective_id=0, has_side_effects=True),
-    )(connectivity, count, fields, density, moduli, metric_diag, metric_cross, extension,
+    )(connectivity.T, count, fields, density, moduli, metric_diag, metric_cross, extension.T,
       jnp.asarray(inner), jnp.asarray(outer))
 
 

time: 23.7 us -> 18.6 us (0.78)
  local copies, waits for them, and re-layouts: 4.69 us -> 0.84 us
  Pallas kernels: 18 us -> 16.9 us
    unnamed x3 -> x1, local copies, waits for them, and re-layouts: 4.69 us -> 0.84 us
    pallas_call x1, Pallas kernels: 18 us -> 16.9 us  [shards(): pl.pallas_call(functools.partial(kernel, total, subs, group), out_shape=p...]
where the time goes in v2:
time: 18.6 us; the launch traced here: 18.4 us
  Pallas kernels  16.9 us (91%)
  local copies, waits for them, and re-layouts  0.84 us (5%)
  between operations  0.66 us (4%)
    pallas_call x1, Pallas kernels, shards(): pl.pallas_call(functools.partial(kernel, total, subs, group), out_shape=p...  16.9 us
    unnamed x1, local copies, waits for them, and re-layouts  0.84 us

profile of v2, /device:TPU:0, one launch (start us, length us, event | category | flops | bytes accessed | tf_op | source)
XLA Modules:
  0.0 18.4 jit_solution(17295865783880902661)
XLA Ops:
  0.7 16.9 %shard_map.100 = f32[5,2,128,128]{3,2,1,0:T(8,128)S(1)} custom-call(s32[3,8]{1,0:T(4,128)} %bitcast.3, s32[1]{0:T(128)S(6)} %copy.13.count, f32[5,2,128,128]{3,2,1,0:T(8,128)} %fields_hbm.1, f32[2,128,128]{2,1,0:T(8,128)} %density_hbm.1, f32[2,2,128,128]{3,2,1,0:T(8,128)} %moduli_hbm.1, f32[2,2,128,128]{3,2,1,0:T(8,128)} %diag_hbm.1, ...), custom_call_target="tpu_custom_call" | custom-call | tf_op jit(solution)/shard_map/pallas_call | solution.py:370
  17.5 0.8 %copy.12 = f32[5,2,128,128]{3,2,1,0:T(8,128)} copy(f32[5,2,128,128]{3,2,1,0:T(8,128)S(1)} %shard_map.100) | data formatting | bytes 1310720

commit v3 on v2

--- a/solution.py
+++ b/solution.py
@@ -115,7 +115,7 @@
             cols[rows, :] = acc
             return _
 
-        lax.fori_loop(0, chunks, columns, 0, unroll=4)
+        lax.fori_loop(0, chunks, columns, 0, unroll=chunks)
         trans[...] = jnp.transpose(cols[...])
         for p in range(slots):
             lines[p * 4 + 2] = trans[pl.ds(p * 16 + 1, 8, stride=2), :]
@@ -198,7 +198,7 @@
                 rate[4, p, rows, :] = shear * (gy[0] + gx[1])
                 return _
 
-            lax.fori_loop(0, chunks, body, 0, unroll=4)
+            lax.fori_loop(0, chunks, body, 0, unroll=chunks)
 
     def add_rows(rate, jump):
         for p in range(slots):
@@ -255,7 +255,7 @@
             return jnp.maximum(top, speed)
 
         part = lax.fori_loop(
-            0, chunks, speeds, jnp.zeros((ROWS, n), jnp.float32), unroll=4
+            0, chunks, speeds, jnp.zeros((ROWS, n), jnp.float32), unroll=chunks
         )
         top = jnp.maximum(top, jnp.where(count[0] > p, part, 0.0))
 
@@ -317,7 +317,7 @@
             rate1[f, p, rows, :] = rate1[f, p, rows, :] + jnp.where(edge, side, 0.0)
         return _
 
-    lax.fori_loop(0, chunks, patch_up, 0, unroll=4)
+    lax.fori_loop(0, chunks, patch_up, 0, unroll=chunks)
     derive(rate1)
     interior(rate2)
 
@@ -347,7 +347,7 @@
                 out_v[f, p, rows, :] = jnp.where(live, value, 0.0)
             return _
 
-        lax.fori_loop(0, chunks, finish, 0, unroll=4)
+        lax.fori_loop(0, chunks, finish, 0, unroll=chunks)
     for copy in sent1 + sent2 + shared1 + shared2:
         copy.wait_send()
 

time: 18.6 us -> 18.1 us (0.973)
  Pallas kernels: 16.9 us -> 16.4 us
    pallas_call x1, Pallas kernels: 16.9 us -> 16.4 us  [shards(): pl.pallas_call(functools.partial(kernel, total, subs, group), out_shape=p...]
where the time goes in v3:
time: 18.1 us; the launch traced here: 17.9 us
  Pallas kernels  16.4 us (91%)
  local copies, waits for them, and re-layouts  0.84 us (5%)
  between operations  0.66 us (4%)
    pallas_call x1, Pallas kernels, shards(): pl.pallas_call(functools.partial(kernel, total, subs, group), out_shape=p...  16.4 us
    unnamed x1, local copies, waits for them, and re-layouts  0.84 us

profile of v3, /device:TPU:0, one launch (start us, length us, event | category | flops | bytes accessed | tf_op | source)
XLA Modules:
  0.0 17.9 jit_solution(8838275217877893059)
XLA Ops:
  0.7 16.4 %shard_map.100 = f32[5,2,128,128]{3,2,1,0:T(8,128)S(1)} custom-call(s32[3,8]{1,0:T(4,128)} %bitcast.3, s32[1]{0:T(128)S(6)} %copy.13.count, f32[5,2,128,128]{3,2,1,0:T(8,128)} %fields_hbm.1, f32[2,128,128]{2,1,0:T(8,128)} %density_hbm.1, f32[2,2,128,128]{3,2,1,0:T(8,128)} %moduli_hbm.1, f32[2,2,128,128]{3,2,1,0:T(8,128)} %diag_hbm.1, ...), custom_call_target="tpu_custom_call" | custom-call | tf_op jit(solution)/shard_map/pallas_call | solution.py:370
  17.0 0.8 %copy.12 = f32[5,2,128,128]{3,2,1,0:T(8,128)} copy(f32[5,2,128,128]{3,2,1,0:T(8,128)S(1)} %shard_map.100) | data formatting | bytes 1310720

commit v4 on v3

--- a/solution.py
+++ b/solution.py
@@ -210,6 +210,10 @@
     lines[...] = jnp.zeros_like(lines)
     lines2[...] = jnp.zeros_like(lines2)
     trans[...] = jnp.zeros_like(trans)
+    loads[0].wait()
+    collect(fld, lines)
+    pl.semaphore_wait(barrier, len(everyone))
+    sent1 = post(lines, outbox1, inbox1, send1, recv1)
     ext_v[...] = jnp.zeros_like(ext_v)
     twice, extra = ext.shape
     ext_v[pl.ds(0, twice), pl.ds(0, extra)] = ext[...]
@@ -230,11 +234,6 @@
     right[...] = jnp.concatenate(
         [jnp.concatenate([hi, lo], axis=1), jnp.concatenate([hi, none], axis=1)], axis=0
     )
-
-    loads[0].wait()
-    collect(fld, lines)
-    pl.semaphore_wait(barrier, len(everyone))
-    sent1 = post(lines, outbox1, inbox1, send1, recv1)
     derive(fld)
 
     for load in loads[1:]:

time: 18.1 us -> 18.1 us (level)
  no operation moved by 1% of the time
where the time goes in v4:
time: 18.1 us; the launch traced here: 17.9 us
  Pallas kernels  16.4 us (91%)
  local copies, waits for them, and re-layouts  0.84 us (5%)
  between operations  0.66 us (4%)
    pallas_call x1, Pallas kernels, shards(): pl.pallas_call(functools.partial(kernel, total, subs, group), out_shape=p...  16.4 us
    unnamed x1, local copies, waits for them, and re-layouts  0.84 us

profile of v4, /device:TPU:0, one launch (start us, length us, event | category | flops | bytes accessed | tf_op | source)
XLA Modules:
  0.0 17.9 jit_solution(6005376803048640267)
XLA Ops:
  0.7 16.4 %shard_map.100 = f32[5,2,128,128]{3,2,1,0:T(8,128)S(1)} custom-call(s32[3,8]{1,0:T(4,128)} %bitcast.3, s32[1]{0:T(128)S(6)} %copy.13.count, f32[5,2,128,128]{3,2,1,0:T(8,128)} %fields_hbm.1, f32[2,128,128]{2,1,0:T(8,128)} %density_hbm.1, f32[2,2,128,128]{3,2,1,0:T(8,128)} %moduli_hbm.1, f32[2,2,128,128]{3,2,1,0:T(8,128)} %diag_hbm.1, ...), custom_call_target="tpu_custom_call" | custom-call | tf_op jit(solution)/shard_map/pallas_call | solution.py:369
  17.0 0.8 %copy.12 = f32[5,2,128,128]{3,2,1,0:T(8,128)} copy(f32[5,2,128,128]{3,2,1,0:T(8,128)S(1)} %shard_map.100) | data formatting | bytes 1310720
